TPU v7x, 32 devices: a whole 2x2x4 slice. The times are simulated.
32 devices in a mesh: frame: 8 (over z, y), clip: 4 (over x, core).
Axes of the slice: x: 2, y: 2, z: 4, core: 2. Of those that a mesh axis runs over, the one named last changes fastest.
Arguments:
- tokens: bfloat16 [4, 64, 2, 49, 256], P('clip', 'frame'), may hold values from -6 to 6
- lengths: int32 [4], P('clip'), may hold values from 32 to 64, as said below
- norm_gain: float32 [256], replicated, may hold values from 0.25 to 1.75
- norm_bias: float32 [256], replicated, may hold values from -1.5 to 1.5
- qkv_weight: float32 [256, 768], replicated, may hold values from -0.375 to 0.375
- qkv_bias: float32 [768], replicated, may hold values from -1.5 to 1.5
- proj_weight: float32 [256, 256], replicated, may hold values from -0.375 to 0.375
- proj_bias: float32 [256], replicated, may hold values from -1.5 to 1.5
- grad_out: bfloat16 [4, 64, 2, 49, 256], P('clip', 'frame'), may hold values from -6 to 6
Outputs:
- mixed: bfloat16 [4, 64, 2, 49, 256], P('clip', 'frame')
- grad_tokens: bfloat16 [4, 64, 2, 49, 256], P('clip', 'frame')
- grad_gain: float32 [256], replicated
- grad_nbias: float32 [256], replicated
- grad_qkv_weight: float32 [256, 768], replicated
- grad_qkv_bias: float32 [768], replicated
- grad_proj_weight: float32 [256, 256], replicated
- grad_proj_bias: float32 [256], replicated
Inputs may be any that keep to these rules, and one draw needn't show every extreme that they name: `lengths`: each clip has at least 32 frames that are not padding, and at least one clip has all 64 frames.
All inputs are finite; a program needn't handle non-finite values.
Results may differ from a plain program's by a relative error of at most 0.012.
Values may be sent and summed in bfloat16 or wider, within the bound.
A program may use at most 192 MiB of HBM per device.

v0:
```python
import jax
import jax.numpy as jnp
from jax import lax
from jax.sharding import PartitionSpec as P

HEADS = 8
WT = 8


def passed_along(array, axis, by):
    devices = lax.axis_size(axis)
    return lax.ppermute(array, axis, [(i, (i + by) % devices) for i in range(devices)])


def branch(
    slab,
    length,
    first_frame,
    frame_total,
    norm_gain,
    norm_bias,
    qkv_weight,
    qkv_bias,
    proj_weight,
    proj_bias,
):
    frames, windows, patch_len, model_width = slab.shape
    head_count = HEADS
    head_depth = model_width // head_count
    offset = WT // 2
    frame_index = jnp.mod(first_frame + jnp.arange(frames, dtype=jnp.int32), frame_total)
    valid_frame = frame_index < length
    region = frame_index < offset
    values = slab.astype(jnp.float32)
    mean_val = jnp.mean(values, axis=-1, keepdims=True)
    variance = jnp.mean((values - mean_val) ** 2, axis=-1, keepdims=True)
    normed = ((values - mean_val) * lax.rsqrt(variance + 1e-05) * norm_gain + norm_bias).astype(
        jnp.bfloat16
    )
    project_qkv = (
        jnp.dot(
            normed.reshape(-1, model_width),
            qkv_weight.astype(jnp.bfloat16),
            preferred_element_type=jnp.float32,
        )
        + qkv_bias
    )
    project_qkv = project_qkv.astype(jnp.bfloat16)
    time_windows = frames // WT
    project_qkv = project_qkv.reshape(
        time_windows, WT, windows, patch_len, 3, head_count, head_depth
    )
    project_qkv = project_qkv.transpose(4, 0, 2, 5, 1, 3, 6).reshape(
        3, time_windows, windows, head_count, WT * patch_len, head_depth
    )
    queries = project_qkv[0].astype(jnp.float32)
    keys_f = project_qkv[1].astype(jnp.float32)
    values_f = project_qkv[2].astype(jnp.float32)
    key_valid = jnp.repeat(valid_frame.reshape(time_windows, WT), patch_len, axis=1)
    key_region = jnp.repeat(region.reshape(time_windows, WT), patch_len, axis=1)
    allowed = key_valid[:, None, :] & (key_region[:, :, None] == key_region[:, None, :])
    scores = jnp.einsum("nwhqe,nwhke->nwhqk", queries, keys_f) * head_depth ** (-0.5)
    scores = jnp.where(allowed[:, None, None], scores, -1000000000.0)
    attn_probs = jax.nn.softmax(scores, axis=-1).astype(jnp.bfloat16)
    attended = jnp.einsum("nwhqk,nwhke->nwhqe", attn_probs.astype(jnp.float32), values_f).astype(
        jnp.bfloat16
    )
    attended = attended.reshape(time_windows, windows, head_count, WT, patch_len, head_depth)
    attended = attended.transpose(0, 3, 1, 4, 2, 5).reshape(-1, model_width)
    projected = (
        jnp.dot(attended, proj_weight.astype(jnp.bfloat16), preferred_element_type=jnp.float32)
        + proj_bias
    )
    projected = (
        projected.reshape(frames, windows, patch_len, model_width)
        * valid_frame.astype(jnp.float32)[:, None, None, None]
    )
    return projected.astype(jnp.bfloat16)


def per_device(
    tokens, lengths, norm_gain, norm_bias, qkv_weight, qkv_bias, proj_weight, proj_bias, grad_out
):
    frames_dev = tokens.shape[1]
    offset = WT // 2
    frame_total = frames_dev * lax.axis_size("frame")
    first_frame = lax.axis_index("frame") * frames_dev
    length = lengths[0]
    params = (norm_gain, norm_bias, qkv_weight, qkv_bias, proj_weight, proj_bias)
    ahead_rows = passed_along(tokens[:, :offset], "frame", -1)
    rolled = jnp.concatenate([tokens[:, offset:], ahead_rows], axis=1)

    def local_fn(slab_in, param_set):
        return branch(slab_in[0], length, first_frame + offset, frame_total, *param_set)[None]

    branch_out, pullback = jax.vjp(local_fn, rolled, params)
    behind = passed_along(branch_out[:, frames_dev - offset :], "frame", 1)
    branch_own = jnp.concatenate([behind, branch_out[:, : frames_dev - offset]], axis=1)
    ahead_grad = passed_along(grad_out[:, :offset], "frame", -1)
    grad_rolled_in = jnp.concatenate([grad_out[:, offset:], ahead_grad], axis=1)
    grad_rolled, grad_params = pullback(grad_rolled_in)
    back_rows = passed_along(grad_rolled[:, frames_dev - offset :], "frame", 1)
    grad_tokens = grad_out + jnp.concatenate(
        [back_rows, grad_rolled[:, : frames_dev - offset]], axis=1
    )
    mixed = (tokens.astype(jnp.float32) + branch_own.astype(jnp.float32)).astype(jnp.bfloat16)
    grad_gain, grad_nbias, grad_qkv_w, grad_qkv_b, grad_proj_w, grad_proj_b = grad_params
    summed = lax.psum(
        (grad_gain, grad_nbias, grad_qkv_w, grad_qkv_b, grad_proj_w, grad_proj_b), ("frame", "clip")
    )
    return (mixed, grad_tokens, summed[0], summed[1], summed[2], summed[3], summed[4], summed[5])


def solution(mesh):
    in_specs = (
        P("clip", "frame", None, None, None),
        P("clip"),
        P(),
        P(),
        P(),
        P(),
        P(),
        P(),
        P("clip", "frame", None, None, None),
    )
    out_specs = (
        P("clip", "frame", None, None, None),
        P("clip", "frame", None, None, None),
        P(),
        P(),
        P(),
        P(),
        P(),
        P(),
    )
    return jax.shard_map(
        per_device, mesh=mesh, in_specs=in_specs, out_specs=out_specs, check_vma=False
    )
```

profile of v0, /device:TPU:1, one launch (start us, length us, event | category | flops | bytes accessed | tf_op | source)
XLA Modules:
  0.0 300.8 jit_solution(15396644120483651811)
XLA Ops:
  8.6 5.1 %collective-permute-start = (bf16[1,4,2,49,256]{4,3,2,1,0:T(8,128)(2,1)S(1)}, bf16[1,4,2,49,256]{4,3,2,1,0:T(8,128)(2,1)S(1)}, u32[]{:S(2)}, u32[]{:S(2)}) collective-permute-start(bf16[1,4,2,49,256]{4,3,2,1,0:T(8,128)(2,1)S(1)} %copy.79), channel_id=1, source_target_pairs={{0,28},{4,0},{8,4},{12,8},{16,12},{20,16},{24,20},{28,24},{1,29},{... | collective-permute-start | bytes 602120 | tf_op jit(solution)/shard_map/ppermute | solution.py:12
  21.1 2.0 add_convert_fusion
  23.1 2.0 copy.52
  30.4 12.6 %reshape.575 = bf16[1,8,2,49,3,8,32]{3,2,1,6,5,4,0:T(2,128)(2,1)S(1)} reshape(bf16[784,768]{0,1:T(8,128)(2,1)} %copy.52) | data formatting | bytes 2408448 | tf_op jit(solution)/shard_map/jvp()/reshape | solution.py:50
  42.9 3.3 %fusion.39 = (bf16[1,1,2,8,8,49,32]{5,2,4,6,3,0,1:T(2,128)(2,1)S(1)}, bf16[1,1,2,8,8,49,32]{5,2,4,6,3,0,1:T(2,128)(2,1)}, bf16[1,1,2,8,8,49,32]{5,2,4,6,3,0,1:T(2,128)(2,1)}) fusion(bf16[3,1,2,8,8,49,32]{5,2,4,6,3,0,1:T(2,128)(2,1)S(1)} %bitcast.82), kind=kLoop, calls=%fused_computation.83 | loop fusion | bytes 2408448 | tf_op jit(solution)/shard_map/jvp()/slice | solution.py:58
  51.5 8.4 %fusion.44 = (f32[2,8,392]{2,1,0:T(8,128)S(1)}, f32[2,8,392,392]{2,3,1,0:T(8,128)}) fusion(pred[392,392]{0,1:T(8,128)(4,1)} %compare_and_fusion, bf16[2,8,392,32]{2,3,1,0:T(8,128)(2,1)S(1)} %reshape.576, bf16[2,8,392,32]{2,3,1,0:T(8,128)(2,1)S(1)} %reshape.577), kind=kOutput, calls=%fused_computation.88 | convolution fusion | flops 167186816 | bytes 10816064 | tf_op jit(solution)/shard_map/jvp()/sub | solution.py:64
  60.0 9.2 %fusion.6 = (f32[2,8,392]{2,1,0:T(8,128)S(1)}, bf16[2,8,392,392]{2,3,1,0:T(8,128)(2,1)}, bf16[2,8,392,392]{2,3,1,0:T(8,128)(2,1)}) fusion(f32[2,8,392,392]{2,3,1,0:T(8,128)} %get-tuple-element.56, f32[2,8,392]{2,1,0:T(8,128)S(1)} %multiply_divide_fusion, f32[2,8,392]{2,1,0:T(8,128)S(1)} %get-tuple-element.55, bf16[2,8,392,32]{2,3,1,0:T(8,128)(2,1)S(1)} %copy-done.2, ...), kind=kOutput, calls=%fused_computation.8 | convolution fusion | flops 174556032 | bytes 20547072 | tf_op jit(solution)/shard_map/transpose(jvp(nwhqk,nwhke->nwhqe))/dot_general | solution.py:65
  69.2 9.9 %fusion.16 = bf16[1,1,2,8,392,32]{4,5,3,2,1,0:T(8,128)(2,1)S(1)} fusion(bf16[2,8,392,32]{2,3,1,0:T(8,128)(2,1)S(1)} %reshape.577, f32[2,8,392,392]{2,3,1,0:T(8,128)} %get-tuple-element.56, bf16[2,8,392,392]{2,3,1,0:T(8,128)(2,1)} %get-tuple-element.57, f32[2,8,392]{2,1,0:T(8,128)S(1)} %neg.15, f32[2,8,392]{2,1,0:T(8,128)S(1)} %get-tuple-element.55, ...), kind=kOutput, calls=%fused_computation.33 | convolution fusion | flops 172304384 | bytes 15758400 | tf_op jit(solution)/shard_map/transpose(jvp(nwhqe,nwhke->nwhqk))/dot_general | solution.py:62
  79.0 8.4 %fusion.15 = bf16[1,1,2,8,392,32]{4,5,3,2,1,0:T(8,128)(2,1)S(1)} fusion(bf16[2,8,392,32]{2,3,1,0:T(8,128)(2,1)S(1)} %reshape.576, f32[2,8,392,392]{2,3,1,0:T(8,128)} %get-tuple-element.56, bf16[2,8,392,392]{2,3,1,0:T(8,128)(2,1)} %get-tuple-element.57, f32[2,8,392]{2,1,0:T(8,128)S(1)} %neg.15, f32[2,8,392]{2,1,0:T(8,128)S(1)} %get-tuple-element.55, ...), kind=kOutput, calls=%fused_computation.32 | convolution fusion | flops 172304384 | bytes 15758400 | tf_op jit(solution)/shard_map/transpose(jvp(nwhqe,nwhke->nwhqk))/dot_general | solution.py:62
  87.5 4.7 %fusion.17 = bf16[1,1,2,8,392,32]{4,5,3,2,1,0:T(8,128)(2,1)S(1)} fusion(bf16[2,8,392,32]{2,3,1,0:T(8,128)(2,1)S(1)} %copy-done.2, bf16[2,8,392,392]{2,3,1,0:T(8,128)(2,1)} %get-tuple-element.37), kind=kOutput, calls=%fused_computation.34 | convolution fusion | flops 157552640 | bytes 5720064 | tf_op jit(solution)/shard_map/transpose(jvp(nwhqk,nwhke->nwhqe))/dot_general | solution.py:65
  92.2 4.8 %convolution_convert_fusion.2 = bf16[2,8,392,32]{2,3,1,0:T(8,128)(2,1)} fusion(bf16[2,8,392,392]{2,3,1,0:T(8,128)(2,1)} %get-tuple-element.37, bf16[2,8,392,32]{2,3,1,0:T(8,128)(2,1)S(1)} %reshape.578), kind=kOutput, calls=%fused_computation.24 | convolution fusion | flops 157552640 | bytes 5720064 | tf_op jit(solution)/shard_map/jvp(nwhqk,nwhke->nwhqe)/dot_general | solution.py:65
  98.3 4.9 %reshape.584 = bf16[3,1,2,8,8,49,32]{5,4,6,3,2,0,1:T(8,128)(2,1)S(1)} reshape(bf16[3,1,2,8,392,32]{4,5,3,2,1,0:T(8,128)(2,1)} %pad_add_fusion) | data formatting | bytes 2408448 | tf_op jit(solution)/shard_map/transpose(jvp())/reshape | solution.py:53
  103.2 6.8 %convert_reduce_fusion = f32[3,8,32]{2,1,0:T(8,128)} fusion(bf16[3,1,2,8,8,49,32]{5,4,6,3,2,0,1:T(8,128)(2,1)S(1)} %reshape.584), kind=kLoop, calls=%fused_computation.16 | loop fusion | flops 1203456 | bytes 1207296 | tf_op jit(solution)/shard_map/transpose(jvp())/reduce_sum | solution.py:41
  110.0 6.6 %copy.83 = bf16[3,1,2,8,8,49,32]{5,2,4,6,3,0,1:T(2,128)(2,1)} copy(bf16[3,1,2,8,8,49,32]{5,4,6,3,2,0,1:T(8,128)(2,1)S(1)} %reshape.584) | data formatting | bytes 2408448 | tf_op jit(solution)/shard_map/transpose(jvp())/reshape | solution.py:53
  116.6 10.1 %reshape.585 = bf16[784,768]{0,1:T(8,128)(2,1)S(1)} reshape(bf16[1,8,2,49,3,8,32]{3,2,1,6,5,4,0:T(2,128)(2,1)} %bitcast.83) | data formatting | bytes 2408448 | tf_op jit(solution)/shard_map/transpose(jvp())/reshape | solution.py:50
  126.7 2.4 fusion.37
  132.5 2.1 reshape.579
  134.6 2.6 copy.84
  137.2 4.0 %reshape.580 = bf16[784,256]{0,1:T(8,128)(2,1)S(1)} reshape(bf16[1,8,2,49,8,32]{3,2,1,5,4,0:T(2,128)(2,1)} %bitcast.85) | data formatting | bytes 802816 | tf_op jit(solution)/shard_map/jvp()/reshape | solution.py:69
  143.6 1.9 fusion.33
  147.8 2.3 multiply_reduce_fusion
  156.3 45.8 %all-reduce.3 = (f32[256]{0:T(256)}, f32[256]{0:T(256)}, f32[768]{0:T(1024)}, f32[256]{0:T(256)}) all-reduce(f32[256]{0:T(256)} %get-tuple-element.24, f32[256]{0:T(256)} %get-tuple-element.26, f32[768]{0:T(1024)S(1)} %reduce_sum.118, f32[256]{0:T(256)} %get-tuple-element.53), channel_id=1, replica_groups=mesh['frame'=8,'clip'=4] {'frame','clip'}, use_global_device_ids=true, to_apply=%region_9.10 | all-reduce | flops 1536 | bytes 12288 | tf_op jit(solution)/shard_map/psum | solution.py:108
  205.6 84.2 %all-reduce.7.cloned.1.call-done = (f32[256,768]{1,0:T(8,128)}, f32[256,256]{1,0:T(8,128)}) async-done(((f32[256,768]{1,0:T(8,128)}, f32[256,256]{1,0:T(8,128)}), (f32[256,768]{1,0:T(8,128)}, f32[256,256]{1,0:T(8,128)})) %all-reduce.7.cloned.1.call-update) | async-done | bytes 1048592 | tf_op jit(solution)/shard_map/psum | solution.py:108
  289.8 2.1 copy.88
  (96 shorter events, 39.1 us)
Async XLA Ops:
  7.2 19.2 %copy-start.5 = (f32[256,256]{1,0:T(8,128)S(1)}, f32[256,256]{1,0:T(8,128)}, u32[]{:S(2)}) copy-start(f32[256,256]{1,0:T(8,128)} %param.15) | copy-start | bytes 786436
  7.2 282.6 %all-reduce.7.cloned.1.call-start = ((), (), s32[]{:S(2)}) async-start(), calls=%async_computation | async-start | bytes 2097152 | tf_op jit(solution)/shard_map/psum | solution.py:108
  8.6 9.4 %collective-permute-start = (bf16[1,4,2,49,256]{4,3,2,1,0:T(8,128)(2,1)S(1)}, bf16[1,4,2,49,256]{4,3,2,1,0:T(8,128)(2,1)S(1)}, u32[]{:S(2)}, u32[]{:S(2)}) collective-permute-start(bf16[1,4,2,49,256]{4,3,2,1,0:T(8,128)(2,1)S(1)} %copy.79), channel_id=1, source_target_pairs={{0,28},{4,0},{8,4},{12,8},{16,12},{20,16},{24,20},{28,24},{1,29},{... | collective-permute-start | bytes 602120 | tf_op jit(solution)/shard_map/ppermute | solution.py:12
  15.1 10.1 %collective-permute-start.2 = (bf16[1,4,2,49,256]{4,3,2,1,0:T(8,128)(2,1)S(1)}, bf16[1,4,2,49,256]{4,3,2,1,0:T(8,128)(2,1)S(1)}, u32[]{:S(2)}, u32[]{:S(2)}) collective-permute-start(bf16[1,4,2,49,256]{4,3,2,1,0:T(8,128)(2,1)S(1)} %copy.81), channel_id=1, source_target_pairs={{0,28},{4,0},{8,4},{12,8},{16,12},{20,16},{24,20},{28,24},{1,29},{... | collective-permute-start | bytes 602120 | tf_op jit(solution)/shard_map/ppermute | solution.py:12
  16.1 26.9 %copy-start.12 = (f32[8]{0:T(128)}, f32[8]{0:T(128)S(1)}, u32[]{:S(2)}) copy-start(f32[8]{0:T(128)S(1)} %get-tuple-element.34) | copy-start | bytes 100
  16.6 9.6 %copy-start.3 = (bf16[1,4,2,49,256]{4,3,2,1,0:T(8,128)(2,1)}, bf16[1,4,2,49,256]{4,3,2,1,0:T(8,128)(2,1)S(1)}, u32[]{:S(2)}) copy-start(bf16[1,4,2,49,256]{4,3,2,1,0:T(8,128)(2,1)S(1)} %copy.82) | copy-start | bytes 602116
  18.0 10.8 %copy-start = (bf16[1,4,2,49,256]{4,3,2,1,0:T(8,128)(2,1)}, bf16[1,4,2,49,256]{4,3,2,1,0:T(8,128)(2,1)S(1)}, u32[]{:S(2)}) copy-start(bf16[1,4,2,49,256]{4,3,2,1,0:T(8,128)(2,1)S(1)} %collective-permute-done) | copy-start | bytes 602116
  18.3 0.6 copy-start.7
  18.7 0.6 copy-start.10
  19.3 0.6 copy-start.9
  25.2 3.7 %copy-start.6 = (bf16[1,4,2,49,256]{4,3,2,1,0:T(8,128)(2,1)}, bf16[1,4,2,49,256]{4,3,2,1,0:T(8,128)(2,1)S(1)}, u32[]{:S(2)}) copy-start(bf16[1,4,2,49,256]{4,3,2,1,0:T(8,128)(2,1)S(1)} %collective-permute-done.2) | copy-start | bytes 602116
  49.3 10.7 %copy-start.2 = (bf16[2,8,392,32]{2,3,1,0:T(8,128)(2,1)S(1)}, bf16[2,8,392,32]{2,3,1,0:T(8,128)(2,1)}, u32[]{:S(2)}) copy-start(bf16[2,8,392,32]{2,3,1,0:T(8,128)(2,1)} %reshape.583) | copy-start | bytes 1204228
  60.0 9.2 %copy-start.8 = (pred[392,392]{0,1:T(8,128)(4,1)S(1)}, pred[392,392]{0,1:T(8,128)(4,1)}, u32[]{:S(2)}) copy-start(pred[392,392]{0,1:T(8,128)(4,1)} %compare_and_fusion) | copy-start | bytes 460996
  92.2 34.6 %copy-start.11 = (f32[256]{0:T(256)S(1)}, f32[256]{0:T(256)}, u32[]{:S(2)}) copy-start(f32[256]{0:T(256)} %param.11) | copy-start | bytes 3076
  116.6 31.2 %copy-start.1 = (bf16[1,4,2,49,256]{4,3,2,1,0:T(8,128)(2,1)S(1)}, bf16[1,4,2,49,256]{4,3,2,1,0:T(8,128)(2,1)}, u32[]{:S(2)}) copy-start(bf16[1,4,2,49,256]{4,3,2,1,0:T(8,128)(2,1)} %copy-done) | copy-start | bytes 602116
  143.5 60.9 %copy-start.4 = (bf16[1,8,2,49,256]{4,2,3,1,0:T(2,128)(2,1)S(1)}, bf16[1,8,2,49,256]{4,2,3,1,0:T(2,128)(2,1)}, u32[]{:S(2)}) copy-start(bf16[1,8,2,49,256]{4,2,3,1,0:T(2,128)(2,1)} %param.17) | copy-start | bytes 1204228
  146.3 55.8 %collective-permute-start.1 = (bf16[1,4,2,49,256]{4,3,2,1,0:T(8,128)(2,1)}, bf16[1,4,2,49,256]{4,3,2,1,0:T(8,128)(2,1)}, u32[]{:S(2)}, u32[]{:S(2)}) collective-permute-start(bf16[1,4,2,49,256]{4,3,2,1,0:T(8,128)(2,1)} %get-tuple-element.47), channel_id=1, source_target_pairs={{0,4},{4,8},{8,12},{12,16},{16,20},{20,24},{24,28},{28,0},{1,5},{5... | collective-permute-start | bytes 602120 | tf_op jit(solution)/shard_map/ppermute | solution.py:12
  156.3 48.2 %collective-permute-start.3 = (bf16[1,4,2,49,256]{4,3,2,1,0:T(8,128)(2,1)S(1)}, bf16[1,4,2,49,256]{4,3,2,1,0:T(8,128)(2,1)S(1)}, u32[]{:S(2)}, u32[]{:S(2)}) collective-permute-start(bf16[1,4,2,49,256]{4,3,2,1,0:T(8,128)(2,1)S(1)} %get-tuple-element.45), channel_id=1, source_target_pairs={{0,4},{4,8},{8,12},{12,16},{16,20},{20,24},{24,28},{28,0},{1,5},{5... | collective-permute-start | bytes 602120 | tf_op jit(solution)/shard_map/ppermute | solution.py:12
Sparse Core Ops, SparseCore 0:
  155.6 134.1 all-reduce.6
where the time goes:
time: 306 us; the launch traced here: 301 us
  waiting for transfers between devices  84.7 us (28%)
  local copies, waits for them, and re-layouts  73.9 us (24%)
  matrix products  53.9 us (18%)
  blocking collectives  45.8 us (15%)
  other arithmetic  20.8 us (7%)
  between operations  15.6 us (5%)
  starting transfers between devices  6.22 us (2%)
    psum x1, waiting for transfers between devices, per_device(): lax.psum((grad_gain, grad_nbias, grad_qkv_w, grad_qkv_b, grad_proj_w, gra...  84.2 us
    psum x1, blocking collectives, per_device(): lax.psum((grad_gain, grad_nbias, grad_qkv_w, grad_qkv_b, grad_proj_w, gra...  45.8 us
    reshape x2, local copies, waits for them, and re-layouts, branch(): project_qkv.reshape(time_windows, WT, windows, patch_len, 3, head_count,...  22.7 us
    dot_general x3, matrix products, branch(): jnp.einsum('nwhqk,nwhke->nwhqe', attn_probs.astype(jnp.float32), values_f)  18.6 us
    dot_general x2, matrix products, branch(): jnp.einsum('nwhqe,nwhke->nwhqk', queries, keys_f) * head_depth ** (-0.5)  18.3 us
    reshape x2, local copies, waits for them, and re-layouts, branch(): project_qkv.transpose(4, 0, 2, 5, 1, 3, 6)  11.5 us
    sub x1, matrix products, branch(): attn_probs = jax.nn.softmax(scores, axis=-1).astype(jnp.bfloat16)  8.44 us
    unnamed x34, local copies, waits for them, and re-layouts  7.18 us
  transfers between devices with their start and end apart: 5, of which 2 were waited for; matrix products, arithmetic and copies ran while one was open for 7% of the time, Pallas kernels for 0%

commit v1 on v0

v1 whole, which is shorter than its diff:
```python
import functools

import jax
import jax.numpy as jnp
from jax import lax
from jax.experimental import pallas as pl
from jax.experimental.pallas import tpu as pltpu
from jax.sharding import PartitionSpec as P

HEADS = 8
WT = 8
MESH = pl.DeviceIdType.MESH
F32 = jnp.float32
BF16 = jnp.bfloat16


def dot(a, b):
    return jnp.dot(a, b, preferred_element_type=F32)


def dot_nt(a, b):
    return lax.dot_general(a, b, (((1,), (1,)), ((), ())), preferred_element_type=F32)


def compute_kernel(
    patch,
    scal,
    x_own,
    x_ahead,
    g_own,
    g_ahead,
    gain,
    nbias,
    wqkv,
    bqkv,
    wproj,
    bproj,
    b_keep,
    b_send,
    d_keep,
    d_send,
    big,
    small,
    xs,
    gs,
    wq16,
    wp16,
    mask,
    probs,
    q16,
    k16,
    v16,
    qt16,
    kt16,
    vt16,
    do16,
    dot16,
    acc_o,
    acc_q,
    dkt,
    dvt,
    acc_big,
):
    step = pl.program_id(0)
    half = WT // 2
    padded = xs.shape[1]
    rows = WT * padded
    width = xs.shape[2]
    depth = width // HEADS
    scale = depth ** (-0.5)
    length = scal[0].astype(F32)
    first = scal[1].astype(F32)
    total = scal[2].astype(F32)
    far = F32(-1e9)

    def frame_of(index):
        row = index.astype(F32)
        slot = jnp.floor((row + 0.5) * (1.0 / padded))
        time = first + slot
        time = jnp.where(time >= total, time - total, time)
        return time, row - slot * padded

    t_col, in_col = frame_of(lax.broadcasted_iota(jnp.int32, (rows, 1), 0))
    valid_col = jnp.where(t_col < length, 1.0, 0.0).astype(F32)

    @pl.when(step == 0)
    def _():
        xs[...] = jnp.zeros_like(xs)
        gs[...] = jnp.zeros_like(gs)
        wq16[...] = wqkv[...].astype(BF16)
        wp16[...] = wproj[...].astype(BF16)
        acc_big[...] = jnp.zeros_like(acc_big)
        small[...] = jnp.zeros_like(small)
        t_row, in_row = frame_of(lax.broadcasted_iota(jnp.int32, (1, rows), 1))
        key_bias = jnp.where((t_row < length) & (in_row < patch), 0.0, far)
        region_row = jnp.where(t_row < half, 1.0, 0.0)
        region_col = jnp.where(t_col < half, 1.0, 0.0)
        mask[...] = key_bias + jnp.where(region_col == region_row, 0.0, far)

    xs[0:half, 0:patch, :] = x_own[0, :, 0].astype(F32)
    xs[half:WT, 0:patch, :] = x_ahead[0, :, 0].astype(F32)
    gs[0:half, 0:patch, :] = g_own[0, :, 0].astype(F32)
    gs[half:WT, 0:patch, :] = g_ahead[0, :, 0].astype(F32)

    x = xs[...].reshape(rows, width)
    mean = jnp.sum(x, axis=-1, keepdims=True) * (1.0 / width)
    xc = x - mean
    var = jnp.sum(xc * xc, axis=-1, keepdims=True) * (1.0 / width)
    inv = lax.rsqrt(var + 1e-05)
    normed_f = (xc * inv * gain[...] + nbias[...]).astype(BF16).astype(F32)
    normed = normed_f.astype(BF16)
    normed_t = normed_f.T.astype(BF16)
    for part, (ref, ref_t) in enumerate(((q16, qt16), (k16, kt16), (v16, vt16))):
        cols = slice(part * width, (part + 1) * width)
        value = dot(normed, wq16[:, cols]) + bqkv[:, cols]
        rounded = value.astype(BF16)
        ref[...] = rounded
        ref_t[...] = rounded.astype(F32).T.astype(BF16)

    lane_head = lax.broadcasted_iota(jnp.int32, (1, width), 1) // depth
    row_head = lax.broadcasted_iota(jnp.int32, (width, 1), 0) // depth
    zero16 = jnp.zeros((), BF16)

    acc_o[...] = jnp.zeros_like(acc_o)

    def forward(h, carry):
        row_on = jnp.where(row_head == h, 1.0, 0.0).astype(BF16)
        lane_on = jnp.where(lane_head == h, 1.0, 0.0).astype(BF16)
        scores = dot(q16[...], kt16[...] * row_on) * scale + mask[...]
        top = jnp.max(scores, axis=-1, keepdims=True)
        e = jnp.exp(scores - top)
        p = (e * (1.0 / jnp.sum(e, axis=-1, keepdims=True))).astype(BF16)
        probs[h] = p
        acc_o[...] += dot(p, v16[...] * lane_on)
        return carry

    lax.fori_loop(0, HEADS, forward, 0, unroll=2)
    att = acc_o[...].astype(BF16)
    att_f = att.astype(F32)
    projected = (dot(att, wp16[...]) + bproj[...]) * valid_col
    projected = projected.reshape(WT, padded, width)
    b_keep[0, :, 0] = projected[0:half, 0:patch].astype(BF16)
    b_send[0, :, 0] = projected[half:WT, 0:patch].astype(BF16)

    g = gs[...].reshape(rows, width) * valid_col
    g_16 = g.astype(BF16)
    small[5:6, :] += jnp.sum(g, axis=0, keepdims=True)
    acc_big[3 * width : 4 * width, :] += dot(att_f.T.astype(BF16), g_16)
    d_att = dot_nt(g_16, wp16[...]).astype(BF16)
    do16[...] = d_att
    d_att_f = d_att.astype(F32)
    dot16[...] = d_att_f.T.astype(BF16)
    acc_o[...] = d_att_f * att_f
    acc_q[...] = jnp.zeros_like(acc_q)

    def backward(h, carry):
        row_on = jnp.where(row_head == h, 1.0, 0.0).astype(BF16)
        lane_on = jnp.where(lane_head == h, 1.0, 0.0).astype(BF16)
        delta = jnp.sum(
            jnp.where(lane_head == h, acc_o[...], 0.0), axis=-1, keepdims=True
        )
        p = probs[h]
        dp = dot(do16[...], vt16[...] * row_on)
        ds = (p.astype(F32) * (dp - delta)).astype(BF16)
        acc_q[...] += dot(ds, k16[...] * lane_on)
        at = pl.ds(pl.multiple_of(h * depth, depth), depth)
        dkt[at, :] = dot(qt16[at, :], ds)
        dvt[at, :] = dot(dot16[at, :], p)
        return carry

    lax.fori_loop(0, HEADS, backward, 0, unroll=2)
    d_normed = jnp.zeros((rows, width), F32)
    for part in range(3):
        if part == 0:
            d_part = acc_q[...] * scale
        elif part == 1:
            d_part = dkt[...].T * scale
        else:
            d_part = dvt[...].T
        d_16 = d_part.astype(BF16)
        cols = slice(part * width, (part + 1) * width)
        small[2 + part : 3 + part, :] += jnp.sum(d_16.astype(F32), axis=0, keepdims=True)
        acc_big[cols, :] += dot(normed_t, d_16)
        d_normed = d_normed + dot_nt(d_16, wq16[:, cols])
    dn = d_normed.astype(BF16).astype(F32)
    x = xs[...].reshape(rows, width)
    xhat = (x - mean) * inv
    small[0:1, :] += jnp.sum(dn * xhat, axis=0, keepdims=True)
    small[1:2, :] += jnp.sum(dn, axis=0, keepdims=True)
    dh = dn * gain[...]
    m1 = jnp.sum(dh, axis=-1, keepdims=True) * (1.0 / width)
    m2 = jnp.sum(dh * xhat, axis=-1, keepdims=True) * (1.0 / width)
    dx = (inv * (dh - m1 - xhat * m2)).reshape(WT, padded, width)
    d_keep[0, :, 0] = dx[0:half, 0:patch].astype(BF16)
    d_send[0, :, 0] = dx[half:WT, 0:patch].astype(BF16)

    @pl.when(step == pl.num_programs(0) - 1)
    def _():
        big[...] = acc_big[...].astype(BF16)


def compute(scal, tokens, ahead, grad_out, ahead_grad, params):
    gain, nbias, wqkv, bqkv, wproj, bproj = params
    _, frames, windows, patch, width = tokens.shape
    half = WT // 2
    padded = -(-patch // 8) * 8
    rows = WT * padded
    own = pl.BlockSpec((1, half, 1, patch, width), lambda w: (0, 1, w, 0, 0))
    other = pl.BlockSpec((1, half, 1, patch, width), lambda w: (0, 0, w, 0, 0))

    def whole(shape):
        return pl.BlockSpec(shape, lambda w: (0,) * len(shape))

    half_shape = jax.ShapeDtypeStruct((1, half, windows, patch, width), BF16)
    tall = pltpu.VMEM((rows, width), BF16)
    wide = pltpu.VMEM((width, rows), BF16)
    return pl.pallas_call(
        functools.partial(compute_kernel, patch),
        grid=(windows,),
        out_shape=[half_shape] * 4
        + [
            jax.ShapeDtypeStruct((4 * width, width), BF16),
            jax.ShapeDtypeStruct((8, width), F32),
        ],
        in_specs=[
            pl.BlockSpec(memory_space=pltpu.SMEM),
            own,
            other,
            own,
            other,
            whole((1, width)),
            whole((1, width)),
            whole((width, 3 * width)),
            whole((1, 3 * width)),
            whole((width, width)),
            whole((1, width)),
        ],
        out_specs=[other] * 4 + [whole((4 * width, width)), whole((8, width))],
        scratch_shapes=[
            pltpu.VMEM((WT, padded, width), F32),
            pltpu.VMEM((WT, padded, width), F32),
            pltpu.VMEM((width, 3 * width), BF16),
            pltpu.VMEM((width, width), BF16),
            pltpu.VMEM((rows, rows), F32),
            pltpu.VMEM((HEADS, rows, rows), BF16),
            tall,
            tall,
            tall,
            wide,
            wide,
            wide,
            tall,
            wide,
            pltpu.VMEM((rows, width), F32),
            pltpu.VMEM((rows, width), F32),
            pltpu.VMEM((width, rows), F32),
            pltpu.VMEM((width, rows), F32),
            pltpu.VMEM((4 * width, width), F32),
        ],
        compiler_params=pltpu.CompilerParams(
            dimension_semantics=("arbitrary",), vmem_limit_bytes=56 * 2**20
        ),
        name="window_attention",
    )(
        scal,
        tokens,
        ahead,
        grad_out,
        ahead_grad,
        gain.reshape(1, width),
        nbias.reshape(1, width),
        wqkv,
        bqkv.reshape(1, 3 * width),
        wproj,
        bproj.reshape(1, width),
    )


def halo_kernel(n_frame, tokens, grads, got_tokens, got_grads, send_sem, recv_sem):
    frame, clip = lax.axis_index("frame"), lax.axis_index("clip")
    before = (lax.rem(frame + n_frame - 1, n_frame), clip)
    after = (lax.rem(frame + 1, n_frame), clip)
    barrier = pltpu.get_barrier_semaphore()
    for peer in (before, after):
        pl.semaphore_signal(barrier, inc=1, device_id=peer, device_id_type=MESH)
    pl.semaphore_wait(barrier, 2)
    half = WT // 2
    copies = []
    for i, (src, dst) in enumerate(((tokens, got_tokens), (grads, got_grads))):
        copy = pltpu.make_async_remote_copy(
            src_ref=src.at[:, 0:half],
            dst_ref=dst,
            send_sem=send_sem.at[i],
            recv_sem=recv_sem.at[i],
            device_id=before,
            device_id_type=MESH,
        )
        copy.start()
        copies.append(copy)
    for copy in copies:
        copy.wait()


def halo(tokens, grad_out, n_frame):
    _, _, windows, patch, width = tokens.shape
    shape = jax.ShapeDtypeStruct((1, WT // 2, windows, patch, width), BF16)
    anywhere = pl.BlockSpec(memory_space=pl.ANY)
    return pl.pallas_call(
        functools.partial(halo_kernel, n_frame),
        out_shape=[shape, shape],
        in_specs=[anywhere] * 2,
        out_specs=[anywhere] * 2,
        scratch_shapes=[pltpu.SemaphoreType.DMA((2,)), pltpu.SemaphoreType.DMA((2,))],
        compiler_params=pltpu.CompilerParams(collective_id=0, has_side_effects=True),
        name="halo",
    )(tokens, grad_out)


def finish_kernel(
    n_frame,
    n_clip,
    branch,
    grads,
    big,
    small,
    got_branch,
    got_grads,
    out_big,
    out_small,
    clip_recv,
    clip_small,
    clip_sum,
    frame_recv,
    frame_small,
    piece,
    h_send,
    h_recv,
    c_send,
    c_recv,
    f_send,
    f_recv,
    a_send,
    a_recv,
    z_send,
    z_recv,
):
    frame, clip = lax.axis_index("frame"), lax.axis_index("clip")
    after = lax.rem(frame + 1, n_frame)
    barrier = pltpu.get_barrier_semaphore()

    def frame_peer(k):
        return lax.rem(frame + k, n_frame)

    def clip_peer(k):
        return lax.rem(clip + k, n_clip)

    for k in range(1, n_clip):
        pl.semaphore_signal(
            barrier, inc=1, device_id=(frame, clip_peer(k)), device_id_type=MESH
        )
    for k in range(1, n_frame):
        pl.semaphore_signal(
            barrier, inc=1, device_id=(frame_peer(k), clip), device_id_type=MESH
        )
    pl.semaphore_wait(barrier, n_clip + n_frame - 2)

    def send(src, dst, s, r, peer):
        copy = pltpu.make_async_remote_copy(
            src_ref=src,
            dst_ref=dst,
            send_sem=s,
            recv_sem=r,
            device_id=peer,
            device_id_type=MESH,
        )
        copy.start()
        return copy

    first = []
    for k in range(1, n_clip):
        peer = (frame, clip_peer(k))
        first.append(
            send(big.at[clip_peer(k)], clip_recv.at[k - 1], c_send.at[0, k], c_recv.at[0, k], peer)
        )
        first.append(send(small, clip_small.at[clip], c_send.at[1, k], c_recv.at[1, k], peer))
    halos = [
        send(branch, got_branch, h_send.at[0], h_recv.at[0], (after, clip)),
        send(grads, got_grads, h_send.at[1], h_recv.at[1], (after, clip)),
    ]
    clip_small[clip] = small[...]
    for copy in first:
        copy.wait()
    total = big[clip].astype(F32)
    for k in range(1, n_clip):
        total = total + clip_recv[k - 1].astype(F32)
    clip_sum[...] = total.astype(BF16)
    total_small = clip_small[0]
    for k in range(1, n_clip):
        total_small = total_small + clip_small[k]
    frame_small[frame] = total_small

    second = []
    for k in range(1, n_frame):
        peer = (frame_peer(k), clip)
        second.append(
            send(
                clip_sum.at[frame_peer(k)],
                frame_recv.at[k - 1],
                f_send.at[0, k],
                f_recv.at[0, k],
                peer,
            )
        )
        second.append(
            send(
                frame_small.at[frame],
                frame_small.at[frame],
                f_send.at[1, k],
                f_recv.at[1, k],
                peer,
            )
        )
    for copy in second:
        copy.wait()
    total = clip_sum[frame].astype(F32)
    for k in range(1, n_frame):
        total = total + frame_recv[k - 1].astype(F32)
    piece[...] = total.astype(BF16)
    total_small = frame_small[0]
    for k in range(1, n_frame):
        total_small = total_small + frame_small[k]
    out_small[...] = total_small
    out_big[clip, frame] = piece[...]

    third = [
        send(
            piece,
            out_big.at[clip, frame],
            a_send.at[k],
            a_recv.at[k],
            (frame_peer(k), clip),
        )
        for k in range(1, n_frame)
    ]
    for copy in third:
        copy.wait()
    fourth = [
        send(
            out_big.at[clip],
            out_big.at[clip],
            z_send.at[k],
            z_recv.at[k],
            (frame, clip_peer(k)),
        )
        for k in range(1, n_clip)
    ]
    for copy in fourth:
        copy.wait()
    for copy in halos:
        copy.wait()


def finish(branch, grads, big, small, n_frame, n_clip):
    rows, width = big.shape
    part = rows // (n_frame * n_clip)
    big = big.reshape(n_clip, n_frame, part, width)
    anywhere = pl.BlockSpec(memory_space=pl.ANY)
    near = pl.BlockSpec(memory_space=pltpu.VMEM)
    dma = pltpu.SemaphoreType.DMA
    return pl.pallas_call(
        functools.partial(finish_kernel, n_frame, n_clip),
        out_shape=[
            jax.ShapeDtypeStruct(branch.shape, BF16),
            jax.ShapeDtypeStruct(grads.shape, BF16),
            jax.ShapeDtypeStruct(big.shape, BF16),
            jax.ShapeDtypeStruct(small.shape, F32),
        ],
        in_specs=[anywhere, anywhere, near, near],
        out_specs=[anywhere, anywhere, near, near],
        scratch_shapes=[
            pltpu.VMEM((n_clip - 1, n_frame, part, width), BF16),
            pltpu.VMEM((n_clip,) + small.shape, F32),
            pltpu.VMEM((n_frame, part, width), BF16),
            pltpu.VMEM((n_frame - 1, part, width), BF16),
            pltpu.VMEM((n_frame,) + small.shape, F32),
            pltpu.VMEM((part, width), BF16),
            dma((2,)),
            dma((2,)),
            dma((2, n_clip)),
            dma((2, n_clip)),
            dma((2, n_frame)),
            dma((2, n_frame)),
            dma((n_frame,)),
            dma((n_frame,)),
            dma((n_clip,)),
            dma((n_clip,)),
        ],
        compiler_params=pltpu.CompilerParams(collective_id=1, has_side_effects=True),
        name="finish",
    )(branch, grads, big, small)


def per_device(
    tokens, lengths, norm_gain, norm_bias, qkv_weight, qkv_bias, proj_weight, proj_bias, grad_out
):
    frames_dev, width = tokens.shape[1], tokens.shape[-1]
    n_frame, n_clip = lax.axis_size("frame"), lax.axis_size("clip")
    first = lax.axis_index("frame") * frames_dev + WT // 2
    scal = jnp.stack(
        [lengths[0], first.astype(jnp.int32), jnp.int32(frames_dev * n_frame), jnp.int32(0)]
    )
    params = (norm_gain, norm_bias, qkv_weight, qkv_bias, proj_weight, proj_bias)
    ahead, ahead_grad = halo(tokens, grad_out, n_frame)
    b_keep, b_send, d_keep, d_send, big, small = compute(
        scal, tokens, ahead, grad_out, ahead_grad, params
    )
    b_got, d_got, big, small = finish(b_send, d_send, big, small, n_frame, n_clip)
    branch_own = jnp.concatenate([b_got, b_keep], axis=1)
    mixed = (tokens.astype(F32) + branch_own.astype(F32)).astype(BF16)
    grad_tokens = grad_out + jnp.concatenate([d_got, d_keep], axis=1)
    big = big.reshape(4, width, width).astype(F32)
    grad_qkv = big[0:3].transpose(1, 0, 2).reshape(width, 3 * width)
    return (
        mixed,
        grad_tokens,
        small[0],
        small[1],
        grad_qkv,
        small[2:5].reshape(3 * width),
        big[3],
        small[5],
    )


def solution(mesh):
    split = P("clip", "frame", None, None, None)
    in_specs = (split, P("clip"), P(), P(), P(), P(), P(), P(), split)
    out_specs = (split, split, P(), P(), P(), P(), P(), P())
    return jax.shard_map(
        per_device, mesh=mesh, in_specs=in_specs, out_specs=out_specs, check_vma=False
    )
```

time: 306 us -> 86.8 us (0.28); the launches traced: 301 us -> 86.5 us
  waiting for transfers between devices: 84.7 us -> 0 us
  Pallas kernels: 0 us -> 74.5 us
  local copies, waits for them, and re-layouts: 73.9 us -> 8.92 us
  matrix products: 53.9 us -> 0 us
  blocking collectives: 45.8 us -> 0 us
  other arithmetic: 20.8 us -> 1.73 us
  between operations: 15.6 us -> 1.41 us
  starting transfers between devices: 6.22 us -> 0 us
    psum x1 -> x0, waiting for transfers between devices: 84.2 us -> none  [per_device(): lax.psum((grad_gain, grad_nbias, grad_qkv_w, grad_qkv_b, grad_proj_w, gra...]
    pallas_call x0 -> x3, Pallas kernels: none -> 74.5 us  [the longest x1 34.9 us: finish(): pl.pallas_call(functools.partial(finish_kernel, n_frame, n_clip), out_sha...]
    psum x1 -> x0, blocking collectives: 45.8 us -> none  [per_device(): lax.psum((grad_gain, grad_nbias, grad_qkv_w, grad_qkv_b, grad_proj_w, gra...]
    dot_general x11 -> x0, matrix products: 45.4 us -> none  [the longest x3 18.6 us: branch(): jnp.einsum('nwhqk,nwhke->nwhqe', attn_probs.astype(jnp.float32), values_f)]
    reshape x9 -> x2, local copies, waits for them, and re-layouts: 44.7 us -> 1.18 us  [the longest x1 0.6 us: per_device(): small[2:5].reshape(3 * width)]
    reduce_sum x6 -> x0, other arithmetic: 12.8 us -> none  [the longest x1 6.83 us: branch(): jnp.dot(normed.reshape(-1, model_width), qkv_weight.astype(jnp.bfloat16),...]
    sub x1 -> x0, matrix products: 8.44 us -> none  [branch(): attn_probs = jax.nn.softmax(scores, axis=-1).astype(jnp.bfloat16)]
    slice x8 -> x5, local copies, waits for them, and re-layouts: 9.83 us -> 1.63 us  [the longest x1 0.72 us: per_device(): big[3]]
  transfers between devices with their start and end apart: 5 -> 0, of which waited for: 2 -> 0; matrix products, arithmetic and copies ran while one was open for 7% -> 0% of each run, Pallas kernels for 0% -> 0%
where the time goes in v1:
time: 86.8 us; the launch traced here: 86.5 us
  Pallas kernels  74.5 us (86%)
  local copies, waits for them, and re-layouts  8.92 us (10%)
  other arithmetic  1.73 us (2%)
  between operations  1.41 us (2%)
    pallas_call x1, Pallas kernels, finish(): pl.pallas_call(functools.partial(finish_kernel, n_frame, n_clip), out_sha...  34.9 us
    pallas_call x1, Pallas kernels, compute(): pl.pallas_call(functools.partial(compute_kernel, patch), grid=(windows,),...  24.9 us
    pallas_call x1, Pallas kernels, halo(): pl.pallas_call(functools.partial(halo_kernel, n_frame), out_shape=[shape,...  14.7 us
    unnamed x21, local copies, waits for them, and re-layouts  6.11 us

profile of v1, /device:TPU:1, one launch (start us, length us, event | category | flops | bytes accessed | tf_op | source)
XLA Modules:
  0.0 86.5 jit_solution(17290901189012420799)
XLA Ops:
  1.3 0.0 copy-start.7
  1.3 0.6 pad_add_fusion.scal
  1.9 0.1 copy-done.7
  2.0 0.6 reshape.72.bqkv
  2.6 1.9 %copy.26.tokens.x_own = bf16[1,8,2,49,256]{4,3,2,1,0:T(8,128)(2,1)} copy(bf16[1,8,2,49,256]{4,2,3,1,0:T(2,128)(2,1)} %param.9) | data formatting | bytes 802816 | tf_op args[0]
  4.4 0.8 copy.28.grads.g_own
  5.3 14.7 %halo.1 = (bf16[1,4,2,49,256]{4,3,2,1,0:T(8,128)(2,1)}, bf16[1,4,2,49,256]{4,3,2,1,0:T(8,128)(2,1)}) custom-call(bf16[1,8,2,49,256]{4,3,2,1,0:T(8,128)(2,1)} %copy.26.tokens.x_own, bf16[1,8,2,49,256]{4,3,2,1,0:T(8,128)(2,1)} %copy.28.grads.g_own), custom_call_target="tpu_custom_call" | custom-call | tf_op jit(solution)/shard_map/halo/pallas_call | solution.py:308
  19.9 24.9 %window_attention.1 = (bf16[1,4,2,49,256]{4,3,2,1,0:T(8,128)(2,1)}, bf16[1,4,2,49,256]{4,3,2,1,0:T(8,128)(2,1)}, bf16[1,4,2,49,256]{4,3,2,1,0:T(8,128)(2,1)}, bf...) custom-call(s32[4]{0:T(128)} %pad_add_fusion.scal, ...), custom_call_target="tpu_custom_call" | custom-call | tf_op jit(solution)/shard_map/window_attention/pallas_call | solution.py:217
  44.9 0.0 copy-start.1
  44.9 0.0 copy-start.5
  44.9 34.9 %finish.1 = (bf16[1,4,2,49,256]{4,3,2,1,0:T(8,128)(2,1)}, bf16[1,4,2,49,256]{4,3,2,1,0:T(8,128)(2,1)}, bf16[4,8,32,256]{3,2,1,0:T(8,128)(2,1)}, f32[8,256]{1,0:T(8,128)}) custom-call(bf16[1,4,2,49,256]{4,3,2,1,0:T(8,128)(2,1)} %get-tuple-element.22.branch, bf16[1,4,2,49,256]{4,3,2,1,0:T(8,128)(2,1)} %get-tuple-element.23.grads, ...), custom_call_target="tpu_custom_call" | custom-call | tf_op jit(solution)/shard_map/finish/pallas_call | solution.py:470
  79.8 1.0 %add_convert_fusion = bf16[1,8,2,49,256]{4,3,2,1,0:T(8,128)(2,1)S(1)} fusion(bf16[1,4,2,49,256]{4,3,2,1,0:T(8,128)(2,1)S(1)} %copy-done.5, bf16[1,4,2,49,256]{4,3,2,1,0:T(8,128)(2,1)} %get-tuple-element.26, bf16[1,8,2,49,256]{4,2,3,1,0:T(2,128)(2,1)S(1)} %copy-done.1), kind=kLoop, calls=%fused_computation | loop fusion | flops 1003520 | bytes 1204224 | tf_op jit(solution)/shard_map/convert_element_type | solution.py:519
  80.9 0.0 copy-start.6
  80.9 0.0 copy-start.3
  80.9 0.0 copy-start.4
  80.9 1.1 %copy.33 = bf16[1,8,2,49,256]{4,2,3,1,0:T(2,128)(2,1)} copy(bf16[1,8,2,49,256]{4,3,2,1,0:T(8,128)(2,1)S(1)} %add_convert_fusion) | data formatting | bytes 802816
  82.0 0.6 fusion
  82.5 0.6 reshape.76
  83.1 0.1 maximum_add_fusion
  83.3 1.1 %copy.34 = bf16[1,8,2,49,256]{4,2,3,1,0:T(2,128)(2,1)} copy(bf16[1,8,2,49,256]{4,3,2,1,0:T(8,128)(2,1)S(1)} %maximum_add_fusion) | data formatting | bytes 802816
  84.3 0.7 slice.30
  85.0 0.1 slice.29
  85.1 0.3 copy.32
  85.4 1.1 %copy.35 = f32[256,768]{1,0:T(8,128)} copy(f32[256,768]{0,1:T(8,128)S(1)} %bitcast.14) | data formatting | bytes 1572864
  (10 shorter events, 0.0 us)
Async XLA Ops:
  1.3 0.7 copy-start.7
  2.6 1.9 %copy-start.2 = (bf16[1,8,2,49,256]{4,2,3,1,0:T(2,128)(2,1)S(1)}, bf16[1,8,2,49,256]{4,2,3,1,0:T(2,128)(2,1)}, u32[]{:S(2)}) copy-start(bf16[1,8,2,49,256]{4,2,3,1,0:T(2,128)(2,1)} %param.17) | copy-start | bytes 1204228
  44.9 34.9 %copy-start.1 = (bf16[1,8,2,49,256]{4,2,3,1,0:T(2,128)(2,1)S(1)}, bf16[1,8,2,49,256]{4,2,3,1,0:T(2,128)(2,1)}, u32[]{:S(2)}) copy-start(bf16[1,8,2,49,256]{4,2,3,1,0:T(2,128)(2,1)} %param.9) | copy-start | bytes 1204228
  44.9 34.9 %copy-start.5 = (bf16[1,4,2,49,256]{4,3,2,1,0:T(8,128)(2,1)S(1)}, bf16[1,4,2,49,256]{4,3,2,1,0:T(8,128)(2,1)}, u32[]{:S(2)}) copy-start(bf16[1,4,2,49,256]{4,3,2,1,0:T(8,128)(2,1)} %get-tuple-element.27) | copy-start | bytes 602116
  80.9 1.1 %copy-start.6 = (f32[8,256]{1,0:T(8,128)S(1)}, f32[8,256]{1,0:T(8,128)}, u32[]{:S(2)}) copy-start(f32[8,256]{1,0:T(8,128)} %get-tuple-element.30) | copy-start | bytes 24580
  80.9 2.3 %copy-start.3 = (bf16[1,4,2,49,256]{4,3,2,1,0:T(8,128)(2,1)S(1)}, bf16[1,4,2,49,256]{4,3,2,1,0:T(8,128)(2,1)}, u32[]{:S(2)}) copy-start(bf16[1,4,2,49,256]{4,3,2,1,0:T(8,128)(2,1)} %get-tuple-element.29) | copy-start | bytes 602116
  80.9 2.3 %copy-start.4 = (bf16[1,4,2,49,256]{4,3,2,1,0:T(8,128)(2,1)S(1)}, bf16[1,4,2,49,256]{4,3,2,1,0:T(8,128)(2,1)}, u32[]{:S(2)}) copy-start(bf16[1,4,2,49,256]{4,3,2,1,0:T(8,128)(2,1)} %get-tuple-element.28) | copy-start | bytes 602116
  83.2 1.1 %copy-start = (bf16[4,8,32,256]{3,2,1,0:T(8,128)(2,1)S(1)}, bf16[4,8,32,256]{3,2,1,0:T(8,128)(2,1)}, u32[]{:S(2)}) copy-start(bf16[4,8,32,256]{3,2,1,0:T(8,128)(2,1)} %get-tuple-element.31) | copy-start | bytes 1572868

commit v2 on v1

--- a/solution.py
+++ b/solution.py
@@ -24,11 +24,12 @@
 
 def compute_kernel(
     patch,
+    n_frame,
     scal,
     x_own,
-    x_ahead,
     g_own,
-    g_ahead,
+    tokens,
+    grads,
     gain,
     nbias,
     wqkv,
@@ -36,11 +37,17 @@
     wproj,
     bproj,
     b_keep,
-    b_send,
     d_keep,
     d_send,
     big,
     small,
+    b_got,
+    ahead,
+    b_send,
+    in_send,
+    in_recv,
+    out_send,
+    out_recv,
     xs,
     gs,
     wq16,
@@ -72,6 +79,40 @@
     first = scal[1].astype(F32)
     total = scal[2].astype(F32)
     far = F32(-1e9)
+    windows = tokens.shape[2]
+    frame, clip = lax.axis_index("frame"), lax.axis_index("clip")
+    before = (lax.rem(frame + n_frame - 1, n_frame), clip)
+    after = (lax.rem(frame + 1, n_frame), clip)
+
+    def incoming(which, w):
+        return pltpu.make_async_remote_copy(
+            src_ref=(tokens, grads)[which].at[0, 0:half, w],
+            dst_ref=ahead.at[which, w],
+            send_sem=in_send.at[which, w],
+            recv_sem=in_recv.at[which, w],
+            device_id=before,
+            device_id_type=MESH,
+        )
+
+    def outgoing(w):
+        return pltpu.make_async_remote_copy(
+            src_ref=b_send.at[w],
+            dst_ref=b_got.at[0, :, w],
+            send_sem=out_send.at[w],
+            recv_sem=out_recv.at[w],
+            device_id=after,
+            device_id_type=MESH,
+        )
+
+    @pl.when(step == 0)
+    def _():
+        barrier = pltpu.get_barrier_semaphore()
+        for peer in (before, after):
+            pl.semaphore_signal(barrier, inc=1, device_id=peer, device_id_type=MESH)
+        pl.semaphore_wait(barrier, 2)
+        for w in range(windows):
+            for which in range(2):
+                incoming(which, w).start()
 
     def frame_of(index):
         row = index.astype(F32)
@@ -98,9 +139,9 @@
         mask[...] = key_bias + jnp.where(region_col == region_row, 0.0, far)
 
     xs[0:half, 0:patch, :] = x_own[0, :, 0].astype(F32)
-    xs[half:WT, 0:patch, :] = x_ahead[0, :, 0].astype(F32)
     gs[0:half, 0:patch, :] = g_own[0, :, 0].astype(F32)
-    gs[half:WT, 0:patch, :] = g_ahead[0, :, 0].astype(F32)
+    incoming(0, step).wait()
+    xs[half:WT, 0:patch, :] = ahead[0, step].astype(F32)
 
     x = xs[...].reshape(rows, width)
     mean = jnp.sum(x, axis=-1, keepdims=True) * (1.0 / width)
@@ -140,12 +181,15 @@
     projected = (dot(att, wp16[...]) + bproj[...]) * valid_col
     projected = projected.reshape(WT, padded, width)
     b_keep[0, :, 0] = projected[0:half, 0:patch].astype(BF16)
-    b_send[0, :, 0] = projected[half:WT, 0:patch].astype(BF16)
+    b_send[step] = projected[half:WT, 0:patch].astype(BF16)
+    outgoing(step).start()
+    incoming(1, step).wait()
+    gs[half:WT, 0:patch, :] = ahead[1, step].astype(F32)
 
     g = gs[...].reshape(rows, width) * valid_col
     g_16 = g.astype(BF16)
     small[5:6, :] += jnp.sum(g, axis=0, keepdims=True)
-    acc_big[3 * width : 4 * width, :] += dot(att_f.T.astype(BF16), g_16)
+    acc_big[:, 3 * width : 4 * width] += dot(att_f.T.astype(BF16), g_16)
     d_att = dot_nt(g_16, wp16[...]).astype(BF16)
     do16[...] = d_att
     d_att_f = d_att.astype(F32)
@@ -180,7 +224,7 @@
         d_16 = d_part.astype(BF16)
         cols = slice(part * width, (part + 1) * width)
         small[2 + part : 3 + part, :] += jnp.sum(d_16.astype(F32), axis=0, keepdims=True)
-        acc_big[cols, :] += dot(normed_t, d_16)
+        acc_big[:, cols] += dot(normed_t, d_16)
         d_normed = d_normed + dot_nt(d_16, wq16[:, cols])
     dn = d_normed.astype(BF16).astype(F32)
     x = xs[...].reshape(rows, width)
@@ -197,9 +241,11 @@
     @pl.when(step == pl.num_programs(0) - 1)
     def _():
         big[...] = acc_big[...].astype(BF16)
-
-
-def compute(scal, tokens, ahead, grad_out, ahead_grad, params):
+        for w in range(windows):
+            outgoing(w).wait()
+
+
+def compute(scal, tokens, grad_out, params, n_frame):
     gain, nbias, wqkv, bqkv, wproj, bproj = params
     _, frames, windows, patch, width = tokens.shape
     half = WT // 2
@@ -215,19 +261,20 @@
     tall = pltpu.VMEM((rows, width), BF16)
     wide = pltpu.VMEM((width, rows), BF16)
     return pl.pallas_call(
-        functools.partial(compute_kernel, patch),
+        functools.partial(compute_kernel, patch, n_frame),
         grid=(windows,),
-        out_shape=[half_shape] * 4
+        out_shape=[half_shape] * 3
         + [
-            jax.ShapeDtypeStruct((4 * width, width), BF16),
+            jax.ShapeDtypeStruct((width, 4 * width), BF16),
             jax.ShapeDtypeStruct((8, width), F32),
+            half_shape,
         ],
         in_specs=[
             pl.BlockSpec(memory_space=pltpu.SMEM),
             own,
-            other,
             own,
-            other,
+            pl.BlockSpec(memory_space=pl.ANY),
+            pl.BlockSpec(memory_space=pl.ANY),
             whole((1, width)),
             whole((1, width)),
             whole((width, 3 * width)),
@@ -235,8 +282,19 @@
             whole((width, width)),
             whole((1, width)),
         ],
-        out_specs=[other] * 4 + [whole((4 * width, width)), whole((8, width))],
+        out_specs=[other] * 3
+        + [
+            whole((width, 4 * width)),
+            whole((8, width)),
+            pl.BlockSpec(memory_space=pl.ANY),
+        ],
         scratch_shapes=[
+            pltpu.VMEM((2, windows, half, patch, width), BF16),
+            pltpu.VMEM((windows, half, patch, width), BF16),
+            pltpu.SemaphoreType.DMA((2, windows)),
+            pltpu.SemaphoreType.DMA((2, windows)),
+            pltpu.SemaphoreType.DMA((windows,)),
+            pltpu.SemaphoreType.DMA((windows,)),
             pltpu.VMEM((WT, padded, width), F32),
             pltpu.VMEM((WT, padded, width), F32),
             pltpu.VMEM((width, 3 * width), BF16),
@@ -255,18 +313,21 @@
             pltpu.VMEM((rows, width), F32),
             pltpu.VMEM((width, rows), F32),
             pltpu.VMEM((width, rows), F32),
-            pltpu.VMEM((4 * width, width), F32),
+            pltpu.VMEM((width, 4 * width), F32),
         ],
         compiler_params=pltpu.CompilerParams(
-            dimension_semantics=("arbitrary",), vmem_limit_bytes=56 * 2**20
+            dimension_semantics=("arbitrary",),
+            vmem_limit_bytes=56 * 2**20,
+            collective_id=0,
+            has_side_effects=True,
         ),
         name="window_attention",
     )(
         scal,
         tokens,
-        ahead,
         grad_out,
-        ahead_grad,
+        tokens,
+        grad_out,
         gain.reshape(1, width),
         nbias.reshape(1, width),
         wqkv,
@@ -276,54 +337,12 @@
     )
 
 
-def halo_kernel(n_frame, tokens, grads, got_tokens, got_grads, send_sem, recv_sem):
-    frame, clip = lax.axis_index("frame"), lax.axis_index("clip")
-    before = (lax.rem(frame + n_frame - 1, n_frame), clip)
-    after = (lax.rem(frame + 1, n_frame), clip)
-    barrier = pltpu.get_barrier_semaphore()
-    for peer in (before, after):
-        pl.semaphore_signal(barrier, inc=1, device_id=peer, device_id_type=MESH)
-    pl.semaphore_wait(barrier, 2)
-    half = WT // 2
-    copies = []
-    for i, (src, dst) in enumerate(((tokens, got_tokens), (grads, got_grads))):
-        copy = pltpu.make_async_remote_copy(
-            src_ref=src.at[:, 0:half],
-            dst_ref=dst,
-            send_sem=send_sem.at[i],
-            recv_sem=recv_sem.at[i],
-            device_id=before,
-            device_id_type=MESH,
-        )
-        copy.start()
-        copies.append(copy)
-    for copy in copies:
-        copy.wait()
-
-
-def halo(tokens, grad_out, n_frame):
-    _, _, windows, patch, width = tokens.shape
-    shape = jax.ShapeDtypeStruct((1, WT // 2, windows, patch, width), BF16)
-    anywhere = pl.BlockSpec(memory_space=pl.ANY)
-    return pl.pallas_call(
-        functools.partial(halo_kernel, n_frame),
-        out_shape=[shape, shape],
-        in_specs=[anywhere] * 2,
-        out_specs=[anywhere] * 2,
-        scratch_shapes=[pltpu.SemaphoreType.DMA((2,)), pltpu.SemaphoreType.DMA((2,))],
-        compiler_params=pltpu.CompilerParams(collective_id=0, has_side_effects=True),
-        name="halo",
-    )(tokens, grad_out)
-
-
 def finish_kernel(
     n_frame,
     n_clip,
-    branch,
     grads,
     big,
     small,
-    got_branch,
     got_grads,
     out_big,
     out_small,
@@ -383,10 +402,7 @@
             send(big.at[clip_peer(k)], clip_recv.at[k - 1], c_send.at[0, k], c_recv.at[0, k], peer)
         )
         first.append(send(small, clip_small.at[clip], c_send.at[1, k], c_recv.at[1, k], peer))
-    halos = [
-        send(branch, got_branch, h_send.at[0], h_recv.at[0], (after, clip)),
-        send(grads, got_grads, h_send.at[1], h_recv.at[1], (after, clip)),
-    ]
+    halos = [send(grads, got_grads, h_send.at[0], h_recv.at[0], (after, clip))]
     clip_small[clip] = small[...]
     for copy in first:
         copy.wait()
@@ -460,7 +476,7 @@
         copy.wait()
 
 
-def finish(branch, grads, big, small, n_frame, n_clip):
+def finish(grads, big, small, n_frame, n_clip):
     rows, width = big.shape
     part = rows // (n_frame * n_clip)
     big = big.reshape(n_clip, n_frame, part, width)
@@ -470,13 +486,12 @@
     return pl.pallas_call(
         functools.partial(finish_kernel, n_frame, n_clip),
         out_shape=[
-            jax.ShapeDtypeStruct(branch.shape, BF16),
             jax.ShapeDtypeStruct(grads.shape, BF16),
             jax.ShapeDtypeStruct(big.shape, BF16),
             jax.ShapeDtypeStruct(small.shape, F32),
         ],
-        in_specs=[anywhere, anywhere, near, near],
-        out_specs=[anywhere, anywhere, near, near],
+        in_specs=[anywhere, near, near],
+        out_specs=[anywhere, near, near],
         scratch_shapes=[
             pltpu.VMEM((n_clip - 1, n_frame, part, width), BF16),
             pltpu.VMEM((n_clip,) + small.shape, F32),
@@ -484,8 +499,8 @@
             pltpu.VMEM((n_frame - 1, part, width), BF16),
             pltpu.VMEM((n_frame,) + small.shape, F32),
             pltpu.VMEM((part, width), BF16),
-            dma((2,)),
-            dma((2,)),
+            dma((1,)),
+            dma((1,)),
             dma((2, n_clip)),
             dma((2, n_clip)),
             dma((2, n_frame)),
@@ -497,7 +512,7 @@
         ],
         compiler_params=pltpu.CompilerParams(collective_id=1, has_side_effects=True),
         name="finish",
-    )(branch, grads, big, small)
+    )(grads, big, small)
 
 
 def per_device(
@@ -510,24 +525,20 @@
         [lengths[0], first.astype(jnp.int32), jnp.int32(frames_dev * n_frame), jnp.int32(0)]
     )
     params = (norm_gain, norm_bias, qkv_weight, qkv_bias, proj_weight, proj_bias)
-    ahead, ahead_grad = halo(tokens, grad_out, n_frame)
-    b_keep, b_send, d_keep, d_send, big, small = compute(
-        scal, tokens, ahead, grad_out, ahead_grad, params
-    )
-    b_got, d_got, big, small = finish(b_send, d_send, big, small, n_frame, n_clip)
+    b_keep, d_keep, d_send, big, small, b_got = compute(scal, tokens, grad_out, params, n_frame)
+    d_got, big, small = finish(d_send, big, small, n_frame, n_clip)
     branch_own = jnp.concatenate([b_got, b_keep], axis=1)
     mixed = (tokens.astype(F32) + branch_own.astype(F32)).astype(BF16)
     grad_tokens = grad_out + jnp.concatenate([d_got, d_keep], axis=1)
-    big = big.reshape(4, width, width).astype(F32)
-    grad_qkv = big[0:3].transpose(1, 0, 2).reshape(width, 3 * width)
+    big = big.reshape(width, 4 * width).astype(F32)
     return (
         mixed,
         grad_tokens,
         small[0],
         small[1],
-        grad_qkv,
+        big[:, : 3 * width],
         small[2:5].reshape(3 * width),
-        big[3],
+        big[:, 3 * width :],
         small[5],
     )
 

time: 86.8 us -> 78.2 us (0.901)
  Pallas kernels: 74.5 us -> 65.3 us
  other arithmetic: 1.73 us -> 2.91 us
    pallas_call x2 -> x1, Pallas kernels: 39.6 us -> 34.1 us  [compute(): pl.pallas_call(functools.partial(compute_kernel, patch, n_frame), grid=(w...]
    pallas_call x1, Pallas kernels: 34.9 us -> 31.2 us  [finish(): pl.pallas_call(functools.partial(finish_kernel, n_frame, n_clip), out_sha...]
    unnamed x21 -> x16, local copies, waits for them, and re-layouts: 6.11 us -> 4.96 us
    add x1, other arithmetic: 0.1 us -> 1.03 us  [per_device(): grad_tokens = grad_out + jnp.concatenate([d_got, d_keep], axis=1)]
where the time goes in v2:
time: 78.2 us; the launch traced here: 78 us
  Pallas kernels  65.3 us (84%)
  local copies, waits for them, and re-layouts  8.39 us (11%)
  other arithmetic  2.91 us (4%)
  between operations  1.36 us (2%)
    pallas_call x1, Pallas kernels, compute(): pl.pallas_call(functools.partial(compute_kernel, patch, n_frame), grid=(w...  34.1 us
    pallas_call x1, Pallas kernels, finish(): pl.pallas_call(functools.partial(finish_kernel, n_frame, n_clip), out_sha...  31.2 us
    unnamed x16, local copies, waits for them, and re-layouts  4.96 us

profile of v2, /device:TPU:1, one launch (start us, length us, event | category | flops | bytes accessed | tf_op | source)
XLA Modules:
  0.0 78.0 jit_solution(13181257350237220342)
XLA Ops:
  1.3 0.0 copy-start.5
  1.3 0.6 pad_add_fusion.scal
  1.9 0.1 copy-done.5
  2.0 0.6 reshape.67.bqkv
  2.6 1.9 %copy.17.x_own.tokens = bf16[1,8,2,49,256]{4,3,2,1,0:T(8,128)(2,1)} copy(bf16[1,8,2,49,256]{4,2,3,1,0:T(2,128)(2,1)} %param.9) | data formatting | bytes 802816 | tf_op args[0]
  4.4 0.0 copy-done.1
  4.4 0.8 %copy.19.g_own.grads = bf16[1,8,2,49,256]{4,3,2,1,0:T(8,128)(2,1)} copy(bf16[1,8,2,49,256]{4,2,3,1,0:T(2,128)(2,1)S(1)} %copy-done.1) | data formatting | bytes 802816 | tf_op args[8]
  5.3 34.1 %window_attention.1 = (bf16[1,4,2,49,256]{4,3,2,1,0:T(8,128)(2,1)}, bf16[1,4,2,49,256]{4,3,2,1,0:T(8,128)(2,1)}, bf16[1,4,2,49,256]{4,3,2,1,0:T(8,128)(2,1)}, bf...) custom-call(s32[4]{0:T(128)} %pad_add_fusion.scal, ...), custom_call_target="tpu_custom_call" | custom-call | tf_op jit(solution)/shard_map/window_attention/pallas_call | solution.py:263
  39.4 0.0 copy-done
  39.4 1.2 %add_convert_fusion = bf16[1,8,2,49,256]{4,3,2,1,0:T(8,128)(2,1)S(1)} fusion(bf16[1,4,2,49,256]{4,3,2,1,0:T(8,128)(2,1)} %get-tuple-element.18, bf16[1,4,2,49,256]{4,3,2,1,0:T(8,128)(2,1)} %get-tuple-element.17, bf16[1,8,2,49,256]{4,2,3,1,0:T(2,128)(2,1)S(1)} %copy-done), kind=kLoop, calls=%fused_computation | loop fusion | flops 1003520 | bytes 1204224 | tf_op jit(solution)/shard_map/convert_element_type | solution.py:531
  40.6 1.1 %copy.23 = bf16[1,8,2,49,256]{4,2,3,1,0:T(2,128)(2,1)} copy(bf16[1,8,2,49,256]{4,3,2,1,0:T(8,128)(2,1)S(1)} %add_convert_fusion) | data formatting | bytes 802816
  41.6 31.2 %finish.1 = (bf16[1,4,2,49,256]{4,3,2,1,0:T(8,128)(2,1)}, bf16[4,8,8,1024]{3,2,1,0:T(8,128)(2,1)}, f32[8,256]{1,0:T(8,128)}) custom-call(bf16[1,4,2,49,256]{4,3,2,1,0:T(8,128)(2,1)} %get-tuple-element.19.grads, bf16[4,8,8,1024]{3,2,1,0:T(8,128)(2,1)} %bitcast.11, f32[8,256]{1,0:T(8,128)} %get-tuple-element.21.small), custom_call_target="tpu_custom_call" | custom-call | tf_op jit(solution)/shard_map/finish/pallas_call | solution.py:486
  72.8 0.0 copy-done.3
  72.8 1.0 %maximum_add_fusion = bf16[1,8,2,49,256]{4,3,2,1,0:T(8,128)(2,1)S(1)} fusion(bf16[1,4,2,49,256]{4,3,2,1,0:T(8,128)(2,1)S(1)} %copy-done.3, bf16[1,4,2,49,256]{4,3,2,1,0:T(8,128)(2,1)} %get-tuple-element.22, bf16[1,8,2,49,256]{4,2,3,1,0:T(2,128)(2,1)S(1)} %copy-done.1), kind=kLoop, calls=%fused_computation.2 | loop fusion | flops 401408 | bytes 1204224 | tf_op jit(solution)/shard_map/add | solution.py:532
  73.9 0.0 copy-start.4
  73.9 0.0 copy-start.2
  73.9 1.1 %copy.24 = bf16[1,8,2,49,256]{4,2,3,1,0:T(2,128)(2,1)} copy(bf16[1,8,2,49,256]{4,3,2,1,0:T(8,128)(2,1)S(1)} %maximum_add_fusion) | data formatting | bytes 802816
  75.0 0.0 copy-done.4
  75.0 0.6 fusion
  75.5 0.6 reshape.70
  76.1 0.0 copy-done.2
  76.1 0.1 bitcast_convert_fusion
  76.3 0.7 slice.25
  77.0 0.9 %slice.24 = f32[256,768]{1,0:T(8,128)} slice(f32[256,1024]{1,0:T(8,128)S(1)} %bitcast_convert_fusion), slice={[0:256], [0:768]} | slice | bytes 1572864 | tf_op jit(solution)/shard_map/slice | solution.py:539
  (4 shorter events, 0.0 us)
Async XLA Ops:
  1.3 0.7 copy-start.5
  2.6 1.9 %copy-start.1 = (bf16[1,8,2,49,256]{4,2,3,1,0:T(2,128)(2,1)S(1)}, bf16[1,8,2,49,256]{4,2,3,1,0:T(2,128)(2,1)}, u32[]{:S(2)}) copy-start(bf16[1,8,2,49,256]{4,2,3,1,0:T(2,128)(2,1)} %param.17) | copy-start | bytes 1204228
  5.3 34.1 %copy-start = (bf16[1,8,2,49,256]{4,2,3,1,0:T(2,128)(2,1)S(1)}, bf16[1,8,2,49,256]{4,2,3,1,0:T(2,128)(2,1)}, u32[]{:S(2)}) copy-start(bf16[1,8,2,49,256]{4,2,3,1,0:T(2,128)(2,1)} %param.9) | copy-start | bytes 1204228
  41.6 31.2 %copy-start.3 = (bf16[1,4,2,49,256]{4,3,2,1,0:T(8,128)(2,1)S(1)}, bf16[1,4,2,49,256]{4,3,2,1,0:T(8,128)(2,1)}, u32[]{:S(2)}) copy-start(bf16[1,4,2,49,256]{4,3,2,1,0:T(8,128)(2,1)} %get-tuple-element.23) | copy-start | bytes 602116
  73.9 1.1 %copy-start.4 = (f32[8,256]{1,0:T(8,128)S(1)}, f32[8,256]{1,0:T(8,128)}, u32[]{:S(2)}) copy-start(f32[8,256]{1,0:T(8,128)} %get-tuple-element.24) | copy-start | bytes 24580
  73.9 2.3 %copy-start.2 = (bf16[4,8,8,1024]{3,2,1,0:T(8,128)(2,1)S(1)}, bf16[4,8,8,1024]{3,2,1,0:T(8,128)(2,1)}, u32[]{:S(2)}) copy-start(bf16[4,8,8,1024]{3,2,1,0:T(8,128)(2,1)} %get-tuple-element.25) | copy-start | bytes 1572868
